TPU v7x, 256 devices: a whole 4x4x8 slice. The times are simulated.
256 devices in a mesh: nest: 4 (over y), tile: 64 (over z, x, core).
Axes of the slice: x: 4, y: 4, z: 8, core: 2. Of those that a mesh axis runs over, the one named last changes fastest.
Arguments:
- child_fields: float32 [4, 32, 1536, 3072], P('nest', None, 'tile'), may hold values from -18 to 18
- row_weights: float32 [8, 24], replicated
- col_weights: float32 [3072, 1024], replicated
- nest_offsets: int32 [4, 2], replicated, may hold values from 0 to 1023, as said below
- priority: int32 [1024, 1024], P('tile', 'nest'), may hold values from -1 to 3, as said below
- parent_old: float32 [32, 1024, 1024], P(None, 'tile', 'nest'), may hold values from -6 to 6
- smooth_rate: float32 [32], replicated, may hold values from 0.03 to 0.22
Outputs:
- parent_new: float32 [32, 1024, 1024], P(None, 'tile', 'nest')
Inputs may be any that keep to these rules, and one draw needn't show every extreme that they name: nest_offsets[n, 0] lies in 0 .. 512 and nest_offsets[n, 1] in 0 .. 1023. priority[x, y] is -1 or a nest n with nest_offsets[n, 0] <= y < nest_offsets[n, 0] + 512.
All inputs are finite; a program needn't handle non-finite values.
Results may differ from a plain program's by a relative error of at most 0.000058.
Values sent between devices are 32-bit elements; how exact they have to be, the bound alone decides.
A program may use at most 128 MiB of HBM per device.

v0:
```python
import jax
import jax.numpy as jnp
from jax import lax
from jax.sharding import PartitionSpec as P


def split_up(value, dim, count):
    lengths = value.shape
    blocks = value.reshape(*lengths[:dim], count, lengths[dim] // count, *lengths[dim + 1 :])
    return jnp.moveaxis(blocks, dim, 0)


def piece_ends(length, count):
    unit = 8 if length >= 8 * count else 1
    return [length // unit * k // count * unit for k in range(1, count)]


def laid_out(blocks, dim):
    lengths = list(blocks.shape[1:])
    lengths[dim] *= blocks.shape[0]
    return jnp.moveaxis(blocks, 0, dim).reshape(lengths)


def several_exchanges(value, axis, pieces, split_dim, concat_dim):
    blocks = split_up(value, split_dim, lax.axis_size(axis))
    split_at = max(range(1, max(2, blocks.ndim - 1)), key=lambda d: blocks.shape[d])
    done = []
    for piece in jnp.split(blocks, piece_ends(blocks.shape[split_at], pieces), axis=split_at):
        if piece.size:
            done.append(lax.all_to_all(piece, axis, split_axis=0, concat_axis=0, tiled=True))
    return laid_out(jnp.concatenate(done, axis=split_at), concat_dim)


def extended(value, sides, width):
    edges = {}
    for axis, dim in sides:
        count, length = (lax.axis_size(axis), value.shape[dim])
        up = [(i, (i + 1) % count) for i in range(count)]
        last = lax.slice_in_dim(value, length - width, length, axis=dim)
        leading = lax.slice_in_dim(value, 0, width, axis=dim)
        edges[dim] = (
            lax.ppermute(last, axis, up),
            lax.ppermute(leading, axis, [(b, a) for a, b in up]),
        )
    done = []
    for _, dim in sides:
        low, high = edges[dim]
        around = [(width, width) if d in done else (0, 0) for d in range(value.ndim)]
        value = jnp.concatenate([jnp.pad(low, around), value, jnp.pad(high, around)], axis=dim)
        done.append(dim)
    return value


def per_device(
    child_fields, row_weights, col_weights, nest_offsets, priority, parent_old, smooth_rate
):
    child_block = child_fields[0]
    planes = child_block.shape[0]
    cell_rows = row_weights.shape[0]
    tile_count = lax.axis_size("tile")
    nest_count = lax.axis_size("nest")
    strip_cols = parent_old.shape[1]
    owned_rows = parent_old.shape[2]
    nrows = cell_rows * tile_count
    nest_id = lax.axis_index("nest")
    thinned = jnp.einsum("pr,frc->fpc", row_weights, child_block, precision=lax.Precision.HIGHEST)
    restricted = jnp.einsum("fpc,cx->xfp", thinned, col_weights, precision=lax.Precision.HIGHEST)
    rolled = jnp.roll(restricted, nest_offsets[nest_id, 1], axis=0)
    outgoing = rolled.reshape(rolled.shape[0], planes * cell_rows)
    arrived = lax.all_to_all(outgoing, "tile", split_axis=0, concat_axis=0, tiled=True)
    column_slab = arrived.reshape(tile_count, strip_cols, planes, cell_rows)
    column_slab = column_slab.transpose(2, 1, 0, 3).reshape(planes, strip_cols, nrows)
    framed = jnp.zeros((planes, strip_cols, owned_rows * nest_count), jnp.float32)
    placed = lax.dynamic_update_slice(
        framed, column_slab, (jnp.int32(0), jnp.int32(0), nest_offsets[nest_id, 0])
    )
    received = several_exchanges(placed[None], "nest", 2, 3, 0)
    merged = parent_old
    for nest_num in range(nest_count):
        merged = jnp.where((priority == nest_num)[None], received[nest_num], merged)
    padded = extended(merged, (("nest", 2), ("tile", 1)), 1)
    west_side = padded[:, :-2, 1:-1]
    east_side = padded[:, 2:, 1:-1]
    south_side = padded[:, 1:-1, :-2]
    north_side = padded[:, 1:-1, 2:]
    south_side = jnp.where(
        nest_id == 0, jnp.concatenate([merged[:, :, :1], south_side[:, :, 1:]], axis=2), south_side
    )
    north_side = jnp.where(
        nest_id == nest_count - 1,
        jnp.concatenate([north_side[:, :, :-1], merged[:, :, -1:]], axis=2),
        north_side,
    )
    return merged + smooth_rate[:, None, None] * (
        east_side + west_side + north_side + south_side - 4.0 * merged
    )


def solution(mesh):
    return jax.shard_map(
        per_device,
        mesh=mesh,
        in_specs=(
            P("nest", None, "tile", None),
            P(),
            P(),
            P(),
            P("tile", "nest"),
            P(None, "tile", "nest"),
            P(),
        ),
        out_specs=P(None, "tile", "nest"),
        check_vma=False,
    )
```

profile of v0, /device:TPU:32, one launch (start us, length us, event | category | flops | bytes accessed | tf_op | source)
XLA Modules:
  0.0 146.0 jit_solution(4163988800008172533)
XLA Ops:
  0.0 1.4 constant_dynamic-slice_fusion
  3.5 8.1 %fusion.4 = f32[32,8,3072]{2,1,0:T(8,128)S(1)} fusion(f32[1,32,24,3072]{3,2,1,0:T(8,128)} %param.7, f32[8,24]{1,0:T(8,128)S(1)} %copy-done), kind=kOutput, calls=%fused_computation.4 | convolution fusion | flops 226492416 | bytes 12583680 | tf_op jit(solution)/shard_map/pr,frc->fpc/dot_general | solution.py:66
  11.7 11.2 %fusion.7 = f32[1024,32,8]{0,2,1:T(8,128)S(1)} fusion(f32[32,8,3072]{2,1,0:T(8,128)S(1)} %fusion.4, f32[3072,1024]{1,0:T(8,128)S(1)} %copy-done.1), kind=kOutput, calls=%fused_computation.7 | convolution fusion | flops 9663676416 | bytes 16777216 | tf_op jit(solution)/shard_map/fpc,cx->xfp/dot_general | solution.py:67
  23.6 4.9 %all_to_all.12 = f32[64,16,256]{1,0,2:T(8,128)} reshape(f32[1024,32,8]{0,2,1:T(8,128)S(1)} %fusion.10) | data formatting | bytes 2097152 | tf_op jit(solution)/shard_map/all_to_all | solution.py:70
  28.4 7.1 %copy.18 = f32[64,16,256]{2,1,0:T(8,128)} copy(f32[64,16,256]{1,0,2:T(8,128)} %all_to_all.12) | data formatting | bytes 2097152 | tf_op jit(solution)/shard_map/all_to_all | solution.py:70
  35.5 11.6 %all-to-all-start = ((f32[64,16,256]{2,1,0:T(8,128)}), f32[64,16,256]{2,1,0:T(8,128)S(1)}, u32[]{:S(2)}, u32[]{:S(2)}) async-start(f32[64,16,256]{2,1,0:T(8,128)} %copy.18), calls=%async_computation | async-start | bytes 2097152 | tf_op jit(solution)/shard_map/all_to_all | solution.py:70
  49.1 26.0 %all-to-all-done = f32[64,16,256]{2,1,0:T(8,128)S(1)} async-done(((f32[64,16,256]{2,1,0:T(8,128)}), f32[64,16,256]{2,1,0:T(8,128)S(1)}, u32[]{:S(2)}, u32[]{:S(2)}) %all-to-all-start) | async-done | bytes 1048608 | tf_op jit(solution)/shard_map/all_to_all | solution.py:70
  75.8 2.7 %copy.20 = f32[32,16,64,8]{0,3,2,1:T(8,128)} copy(f32[32,16,64,8]{2,3,0,1:T(8,128)S(1)} %bitcast.50) | data formatting | bytes 2097152 | tf_op jit(solution)/shard_map/transpose | solution.py:72
  78.5 3.0 %copy.21 = f32[32,16,512]{2,1,0:T(8,128)S(1)} copy(f32[32,16,512]{0,2,1:T(8,128)} %bitcast.49) | data formatting | bytes 2097152 | tf_op jit(solution)/shard_map/reshape | solution.py:72
  81.8 6.7 %dynamic_update_slice.3 = f32[32,16,1024]{2,1,0:T(8,128)S(1)} dynamic-update-slice(f32[32,16,1024]{2,1,0:T(8,128)S(1)} %broadcast_in_dim.32, f32[32,16,512]{2,1,0:T(8,128)S(1)} %copy.21, s32[]{:T(128)} %constant.39.clone.1, s32[]{:T(128)} %constant.39.clone.1, s32[]{:T(128)S(6)} %select_n.50) | dynamic-update-slice | bytes 2097156 | tf_op jit(solution)/shard_map/dynamic_update_slice | solution.py:74
  88.5 2.0 %reshape_broadcast_in_dim.3 = f32[1,32,16,4,256]{4,3,2,1,0:T(4,128)} reshape(f32[32,16,1024]{2,1,0:T(8,128)S(1)} %dynamic_update_slice.3) | data formatting | bytes 4194304 | tf_op jit(solution)/shard_map/reshape;broadcast_in_dim | solution.py:9
  90.5 1.9 %fusion.26 = (f32[4,1,16,16,256]{4,0,3,2,1:T(4,128)S(1)}, f32[4,1,16,16,256]{4,0,3,2,1:T(4,128)S(1)}) fusion(f32[4,1,32,16,256]{4,0,3,2,1:T(4,128)} %bitcast.51), kind=kLoop, calls=%fused_computation.46 | loop fusion | bytes 4194304 | tf_op jit(solution)/shard_map/split | solution.py:28
  92.4 1.2 copy.22
  93.6 4.7 %all-to-all-start.1 = ((f32[4,1,16,16,256]{4,3,2,1,0:T(8,128)}), f32[4,1,16,16,256]{4,3,2,1,0:T(8,128)S(1)}, u32[]{:S(2)}, u32[]{:S(2)}) async-start(f32[4,1,16,16,256]{4,3,2,1,0:T(8,128)} %copy.22), calls=%async_computation.1 | async-start | bytes 2097152 | tf_op jit(solution)/shard_map/all_to_all | solution.py:30
  98.3 1.2 copy.23
  99.5 14.3 %all-to-all-done.1 = f32[4,1,16,16,256]{4,3,2,1,0:T(8,128)S(1)} async-done(((f32[4,1,16,16,256]{4,3,2,1,0:T(8,128)}), f32[4,1,16,16,256]{4,3,2,1,0:T(8,128)S(1)}, u32[]{:S(2)}, u32[]{:S(2)}) %all-to-all-start.1) | async-done | bytes 1048608 | tf_op jit(solution)/shard_map/all_to_all | solution.py:30
  113.8 4.3 %all-to-all-start.2 = ((f32[4,1,16,16,256]{4,3,2,1,0:T(8,128)}), f32[4,1,16,16,256]{4,3,2,1,0:T(8,128)}, u32[]{:S(2)}, u32[]{:S(2)}) async-start(f32[4,1,16,16,256]{4,3,2,1,0:T(8,128)} %copy.23), calls=%async_computation.2 | async-start | bytes 2097152 | tf_op jit(solution)/shard_map/all_to_all | solution.py:30
  118.2 14.6 %all-to-all-done.2 = f32[4,1,16,16,256]{4,3,2,1,0:T(8,128)} async-done(((f32[4,1,16,16,256]{4,3,2,1,0:T(8,128)}), f32[4,1,16,16,256]{4,3,2,1,0:T(8,128)}, u32[]{:S(2)}, u32[]{:S(2)}) %all-to-all-start.2) | async-done | bytes 1048608 | tf_op jit(solution)/shard_map/all_to_all | solution.py:30
  132.8 1.3 constant_dynamic-update-slice_fusion
  134.1 1.4 fusion.24
  136.3 2.7 %collective-permute-start.1 = (f32[32,16,1]{2,1,0:T(8,128)S(1)}, f32[32,16,1]{2,1,0:T(8,128)S(1)}, u32[]{:S(2)}, u32[]{:S(2)}) collective-permute-start(f32[32,16,1]{2,1,0:T(8,128)S(1)} %get-tuple-element.11), channel_id=1, source_target_pairs={{64,0},{128,64},{192,128},{0,192},{65,1},{129,65},{193,129},{1,193... | collective-permute-start | bytes 6152 | tf_op jit(solution)/shard_map/ppermute | solution.py:43
  139.7 3.7 %collective-permute-done = f32[32,16,1]{2,1,0:T(8,128)S(1)} collective-permute-done((f32[32,16,1]{2,1,0:T(8,128)S(1)}, f32[32,16,1]{2,1,0:T(8,128)S(1)}, u32[]{:S(2)}, u32[]{:S(2)}) %collective-permute-start) | collective-permute-done | bytes 2080 | tf_op jit(solution)/shard_map/ppermute | solution.py:42
  143.4 1.0 collective-permute-done.3
  144.4 1.6 %fusion.15 = f32[32,16,256]{2,1,0:T(8,128)} fusion(f32[32,16,256]{2,1,0:T(8,128)S(1)} %fusion.24, f32[32,16,1]{2,1,0:T(8,128)S(1)} %collective-permute-done, f32[32,16,1]{2,1,0:T(8,128)S(1)} %collective-permute-done.1, f32[32,1,256]{2,1,0:T(1,128)S(1)} %collective-permute-done.3, f32[32,1,256]{2,1,0:T(1,128)S(1)} %collective-permute-done.2, ...), kind=kLoop, calls=%fused_computation.14 | loop fusion | flops 3276800 | bytes 2166914 | tf_op jit(solution)/shard_map/add | solution.py:94
  (21 shorter events, 3.2 us)
Async XLA Ops:
  0.0 3.5 %copy-start = (f32[8,24]{1,0:T(8,128)S(1)}, f32[8,24]{1,0:T(8,128)}, u32[]{:S(2)}) copy-start(f32[8,24]{1,0:T(8,128)} %param.8) | copy-start | bytes 2308
  3.5 8.1 %copy-start.1 = (f32[3072,1024]{1,0:T(8,128)S(1)}, f32[3072,1024]{1,0:T(8,128)}, u32[]{:S(2)}) copy-start(f32[3072,1024]{1,0:T(8,128)} %param.9) | copy-start | bytes 37748740
  35.5 39.5 %all-to-all-start = ((f32[64,16,256]{2,1,0:T(8,128)}), f32[64,16,256]{2,1,0:T(8,128)S(1)}, u32[]{:S(2)}, u32[]{:S(2)}) async-start(f32[64,16,256]{2,1,0:T(8,128)} %copy.18), calls=%async_computation | async-start | bytes 2097152 | tf_op jit(solution)/shard_map/all_to_all | solution.py:70
  93.6 24.5 %copy-start.2 = (s32[16,256]{1,0:T(8,128)S(1)}, s32[16,256]{1,0:T(8,128)}, u32[]{:S(2)}) copy-start(s32[16,256]{1,0:T(8,128)} %param.11) | copy-start | bytes 49156
  93.6 20.2 %all-to-all-start.1 = ((f32[4,1,16,16,256]{4,3,2,1,0:T(8,128)}), f32[4,1,16,16,256]{4,3,2,1,0:T(8,128)S(1)}, u32[]{:S(2)}, u32[]{:S(2)}) async-start(f32[4,1,16,16,256]{4,3,2,1,0:T(8,128)} %copy.22), calls=%async_computation.1 | async-start | bytes 2097152 | tf_op jit(solution)/shard_map/all_to_all | solution.py:30
  113.8 19.0 %all-to-all-start.2 = ((f32[4,1,16,16,256]{4,3,2,1,0:T(8,128)}), f32[4,1,16,16,256]{4,3,2,1,0:T(8,128)}, u32[]{:S(2)}, u32[]{:S(2)}) async-start(f32[4,1,16,16,256]{4,3,2,1,0:T(8,128)} %copy.23), calls=%async_computation.2 | async-start | bytes 2097152 | tf_op jit(solution)/shard_map/all_to_all | solution.py:30
  134.1 10.3 %copy-start.3 = (f32[32]{0:T(128)S(1)}, f32[32]{0:T(128)}, u32[]{:S(2)}) copy-start(f32[32]{0:T(128)} %param.13) | copy-start | bytes 388
  135.7 7.8 %collective-permute-start = (f32[32,16,1]{2,1,0:T(8,128)S(1)}, f32[32,16,1]{2,1,0:T(8,128)S(1)}, u32[]{:S(2)}, u32[]{:S(2)}) collective-permute-start(f32[32,16,1]{2,1,0:T(8,128)S(1)} %get-tuple-element.12), channel_id=1, source_target_pairs={{0,64},{64,128},{128,192},{192,0},{1,65},{65,129},{129,193},{193,1... | collective-permute-start | bytes 6152 | tf_op jit(solution)/shard_map/ppermute | solution.py:42
  136.3 7.1 %collective-permute-start.1 = (f32[32,16,1]{2,1,0:T(8,128)S(1)}, f32[32,16,1]{2,1,0:T(8,128)S(1)}, u32[]{:S(2)}, u32[]{:S(2)}) collective-permute-start(f32[32,16,1]{2,1,0:T(8,128)S(1)} %get-tuple-element.11), channel_id=1, source_target_pairs={{64,0},{128,64},{192,128},{0,192},{65,1},{129,65},{193,129},{1,193... | collective-permute-start | bytes 6152 | tf_op jit(solution)/shard_map/ppermute | solution.py:43
  139.0 4.4 %collective-permute-start.2 = (f32[32,1,256]{2,1,0:T(1,128)S(1)}, f32[32,1,256]{2,1,0:T(1,128)S(1)}, u32[]{:S(2)}, u32[]{:S(2)}) collective-permute-start(f32[32,1,256]{2,1,0:T(1,128)S(1)} %get-tuple-element.9), channel_id=1, source_target_pairs={{1,0},{2,1},{3,2},{4,3},{5,4},{6,5},{7,6},{8,7},{9,8},{10,9},{11,1... | collective-permute-start | bytes 98312 | tf_op jit(solution)/shard_map/ppermute | solution.py:43
  139.0 5.4 %collective-permute-start.3 = (f32[32,1,256]{2,1,0:T(1,128)S(1)}, f32[32,1,256]{2,1,0:T(1,128)S(1)}, u32[]{:S(2)}, u32[]{:S(2)}) collective-permute-start(f32[32,1,256]{2,1,0:T(1,128)S(1)} %get-tuple-element.10), channel_id=1, source_target_pairs={{0,1},{1,2},{2,3},{3,4},{4,5},{5,6},{6,7},{7,8},{8,9},{9,10},{10,1... | collective-permute-start | bytes 98312 | tf_op jit(solution)/shard_map/ppermute | solution.py:42
where the time goes:
time: 147 us; the launch traced here: 146 us
  waiting for transfers between devices  59.6 us (41%)
  local copies, waits for them, and re-layouts  34.9 us (24%)
  starting transfers between devices  24.4 us (17%)
  matrix products  19.4 us (13%)
  between operations  4.2 us (3%)
  other arithmetic  3.57 us (2%)
    all_to_all x2, waiting for transfers between devices, several_exchanges(): lax.all_to_all(piece, axis, split_axis=0, concat_axis=0, tiled=True)  28.9 us
    all_to_all x1, waiting for transfers between devices, per_device(): lax.all_to_all(outgoing, 'tile', split_axis=0, concat_axis=0, tiled=True)  26 us
    all_to_all x3, local copies, waits for them, and re-layouts, per_device(): lax.all_to_all(outgoing, 'tile', split_axis=0, concat_axis=0, tiled=True)  12.7 us
    all_to_all x1, starting transfers between devices, per_device(): lax.all_to_all(outgoing, 'tile', split_axis=0, concat_axis=0, tiled=True)  11.6 us
    dot_general x1, matrix products, per_device(): jnp.einsum('fpc,cx->xfp', thinned, col_weights, precision=lax.Precision.H...  11.2 us
    all_to_all x2, starting transfers between devices, several_exchanges(): lax.all_to_all(piece, axis, split_axis=0, concat_axis=0, tiled=True)  8.96 us
    dot_general x1, matrix products, per_device(): jnp.einsum('pr,frc->fpc', row_weights, child_block, precision=lax.Precisi...  8.12 us
    dynamic_update_slice x1, local copies, waits for them, and re-layouts, per_device(): lax.dynamic_update_slice(framed, column_slab, (jnp.int32(0), jnp.int32(0)...  6.74 us
  transfers between devices with their start and end apart: 7, of which 5 were waited for; matrix products, arithmetic and copies ran while one was open for 1% of the time, Pallas kernels for 0%

commit v1 on v0

v1 whole, which is shorter than its diff:
```python
import functools

import jax
import jax.numpy as jnp
from jax import lax
from jax.experimental import pallas as pl
from jax.experimental.pallas import tpu as pltpu
from jax.sharding import PartitionSpec as P

MESH = pl.DeviceIdType.MESH
TILES = 64
NESTS = 4
GROUPS = 4
GF = 8
PR = 8
STRIP = 16
LANES = 128
NROWS = 512
OWN = 256
DEPTH = 512


def split(value):
    high = value.astype(jnp.bfloat16)
    low = (value - high.astype(jnp.float32)).astype(jnp.bfloat16)
    return high, low


def dot(a, b):
    return jnp.dot(a, b, preferred_element_type=jnp.float32)


def block_diagonal(weights, fields):
    rows, depth = weights.shape
    shape = (fields * rows, fields * depth)
    left = lax.broadcasted_iota(jnp.int32, (shape[0], rows), 0) % rows
    left = (left == lax.broadcasted_iota(jnp.int32, (shape[0], rows), 1)).astype(jnp.bfloat16)
    right = lax.broadcasted_iota(jnp.int32, (depth, shape[1]), 1) % depth
    right = (right == lax.broadcasted_iota(jnp.int32, (depth, shape[1]), 0)).astype(jnp.bfloat16)
    same = lax.broadcasted_iota(jnp.int32, shape, 0) // rows == lax.broadcasted_iota(jnp.int32, shape, 1) // depth
    spread = dot(dot(left, weights).astype(jnp.bfloat16), right)
    return jnp.where(same, spread, 0.0).astype(jnp.bfloat16)


def regroup(tiles):
    group = lax.broadcasted_iota(jnp.int32, (PR, LANES), 1) // STRIP
    for step in (1, 2, 4):
        keep = (group & step) == 0
        for i in range(GF):
            if i & step == 0:
                a, b = tiles[i], tiles[i + step]
                tiles[i] = jnp.where(keep, a, pltpu.roll(b, STRIP * step, 1))
                tiles[i + step] = jnp.where(keep, pltpu.roll(a, LANES - STRIP * step, 1), b)
    return tiles


def restrict_kernel(shift_ref, child_ref, rw_ref, cw_ref, out_ref, total, rolled):
    step = pl.program_id(0)
    w_high, w_low = split(rw_ref[...])
    w_high, w_low = block_diagonal(w_high, GF), block_diagonal(w_low, GF)
    thin = []
    for g in range(GROUPS):
        c_high, c_low = split(child_ref[pl.ds(g * GF, GF)].reshape(GF * 24, DEPTH))
        thin.append(dot(w_high, c_high) + (dot(w_low, c_high) + dot(w_high, c_low)))
    t_high, t_low = split(jnp.concatenate(thin, axis=0))
    m_high, m_low = split(cw_ref[...])
    part = dot(t_high, m_high) + (dot(t_low, m_high) + dot(t_high, m_low))

    @pl.when(step == 0)
    def _():
        total[...] = part

    @pl.when(step > 0)
    def _():
        total[...] += part

    @pl.when(step == pl.num_programs(0) - 1)
    def _():
        rolled[...] = pltpu.roll(total[...], shift_ref[0], 1)

        @pl.loop(0, GROUPS)
        def _(g):
            for z in range(8):
                tiles = [
                    rolled[pl.ds(pl.multiple_of((g * GF + f) * PR, PR), PR), z * LANES : (z + 1) * LANES]
                    for f in range(GF)
                ]
                for s, tile in enumerate(regroup(tiles)):
                    out_ref[z * 8 + s, g] = tile


def exchange_kernel(
    rate_ref, offsets_ref, sent, priority_ref, old_ref, out_ref,
    slabs, halves, nests, merged, mask, edges, rows_in, edges_in,
    tile_send, tile_recv, nest_send, nest_recv, halo_send, halo_recv,
):
    me, nest = lax.axis_index("tile"), lax.axis_index("nest")
    barrier = pltpu.get_barrier_semaphore()

    @pl.loop(1, TILES)
    def _(d):
        pl.semaphore_signal(barrier, inc=1, device_id={"tile": lax.rem(me + d, TILES)}, device_id_type=MESH)

    for d in range(1, NESTS):
        pl.semaphore_signal(barrier, inc=1, device_id={"nest": lax.rem(nest + d, NESTS)}, device_id_type=MESH)
    pl.semaphore_wait(barrier, TILES - 1 + NESTS - 1)

    own_rows = pl.ds(pl.multiple_of(me * PR, PR), PR)
    for g in range(GROUPS):
        @pl.loop(1, TILES)
        def _(d):
            peer = lax.rem(me + d, TILES)
            pltpu.make_async_remote_copy(
                src_ref=sent.at[peer, g], dst_ref=slabs[g].at[own_rows],
                send_sem=tile_send.at[g], recv_sem=tile_recv.at[g],
                device_id={"tile": peer}, device_id_type=MESH,
            ).start()

    for g in range(GROUPS):
        slabs[g][own_rows, :] = sent[me, g]

    spread = jnp.concatenate([priority_ref[...].astype(jnp.float32)] * GF, axis=0)
    mask[...] = spread.T
    for g in range(GROUPS):
        merged[g] = old_ref[pl.ds(g * GF, GF)].reshape(LANES, OWN).T

    def wait(ref, sem):
        pltpu.make_async_copy(ref, ref, sem).wait()

    first = offsets_ref[nest, 0]
    half = lax.rem(nest, 2)

    def nest_copy(g, d):
        peer = lax.rem(nest + d, NESTS)
        return pltpu.make_async_remote_copy(
            src_ref=halves.at[g, pl.ds(pl.multiple_of(lax.rem(peer, 2) * OWN, OWN), OWN)],
            dst_ref=nests.at[nest, g],
            send_sem=nest_send.at[g, d], recv_sem=nest_recv.at[g, d],
            device_id={"nest": peer}, device_id_type=MESH,
        )

    for g in range(GROUPS):
        wait(slabs[g].at[pl.ds(0, NROWS - PR)], tile_recv.at[g])
        slab = slabs[g]
        slab[NROWS : NROWS + PR, :] = slab[0:PR, :]

        @pl.loop(0, NROWS // PR)
        def _(b):
            start = (b * PR - first) & (NROWS - 1)
            halves[g, pl.ds(pl.multiple_of(b * PR, PR), PR), :] = slab[pl.ds(start, PR), :]

        for d in range(1, NESTS):
            nest_copy(g, d).start()
        nests[nest, g] = halves[g, pl.ds(pl.multiple_of(half * OWN, OWN), OWN), :]

    lane = lax.broadcasted_iota(jnp.int32, (STRIP, LANES), 1)
    column = lane % STRIP
    east, west = lax.rem(me + 1, TILES), lax.rem(me + TILES - 1, TILES)
    above, below = lax.rem(nest + 1, NESTS), lax.rem(nest + NESTS - 1, NESTS)

    def halo_copies(g):
        def copy(src, dst, k, device):
            return pltpu.make_async_remote_copy(
                src_ref=src, dst_ref=dst, send_sem=halo_send.at[g, k], recv_sem=halo_recv.at[g, k],
                device_id=device, device_id_type=MESH,
            )
        return [
            copy(edges.at[0, g], edges_in.at[0, g], 0, {"tile": east}),
            copy(edges.at[1, g], edges_in.at[1, g], 1, {"tile": west}),
            copy(merged.at[g, pl.ds(OWN - PR, PR)], rows_in.at[0, g], 2, {"nest": above}),
            copy(merged.at[g, pl.ds(0, PR)], rows_in.at[1, g], 3, {"nest": below}),
        ]

    for g in range(GROUPS):
        for d in range(1, NESTS):
            nest_copy(g, d).wait_recv()
        high = jnp.zeros((STRIP, LANES), jnp.float32)
        low = jnp.zeros((STRIP, LANES), jnp.float32)
        for b in range(OWN // STRIP):
            rows = slice(b * STRIP, (b + 1) * STRIP)
            chosen = merged[g, rows, :]
            which = mask[rows, :]
            for n in range(NESTS):
                chosen = jnp.where(which == n, nests[n, g, rows, :], chosen)
            merged[g, rows, :] = chosen
            to_high = pltpu.roll(chosen, (b - (STRIP - 1)) % LANES, 1)
            to_low = pltpu.roll(chosen, b, 1)
            high = jnp.where(column == b, to_high, high)
            low = jnp.where(column == b, to_low, low)
        edges[0, g] = high
        edges[1, g] = low
        for copy in halo_copies(g):
            copy.start()

    wide = lax.broadcasted_iota(jnp.int32, (OWN, LANES), 1)
    wide_column = wide % STRIP
    row = lax.broadcasted_iota(jnp.int32, (OWN, LANES), 0)
    for g in range(GROUPS):
        copies = halo_copies(g)
        for copy in copies:
            copy.wait_recv()
        cell = merged[g]
        from_west = edges_in[0, g]
        from_east = edges_in[1, g]
        west_edge = jnp.concatenate(
            [pltpu.roll(from_west, (-b) % LANES, 1) for b in range(OWN // STRIP)], axis=0
        )
        east_edge = jnp.concatenate(
            [pltpu.roll(from_east, (STRIP - 1 - b) % LANES, 1) for b in range(OWN // STRIP)], axis=0
        )
        west_side = jnp.where(wide_column == 0, west_edge, pltpu.roll(cell, 1, 1))
        east_side = jnp.where(wide_column == STRIP - 1, east_edge, pltpu.roll(cell, LANES - 1, 1))
        south_row = jnp.where(nest == 0, cell[0:1], rows_in[0, g, PR - 1 : PR])
        north_row = jnp.where(nest == NESTS - 1, cell[OWN - 1 : OWN], rows_in[1, g, 0:1])
        south_side = jnp.where(row == 0, south_row, pltpu.roll(cell, 1, 0))
        north_side = jnp.where(row == OWN - 1, north_row, pltpu.roll(cell, OWN - 1, 0))
        rate = jnp.full((1, LANES), rate_ref[g * GF], jnp.float32)
        for f in range(1, GF):
            rate = jnp.where(wide[0:1] // STRIP == f, rate_ref[g * GF + f], rate)
        new = cell + rate * (east_side + west_side + north_side + south_side - 4.0 * cell)
        out_ref[pl.ds(g * GF, GF)] = new.T.reshape(GF, STRIP, OWN)

    for g in range(GROUPS):
        wait(slabs[g].at[pl.ds(0, NROWS - PR)], tile_send.at[g])
        for d in range(1, NESTS):
            nest_copy(g, d).wait_send()
        for copy in halo_copies(g):
            copy.wait_send()


def per_device(child_fields, row_weights, col_weights, nest_offsets, priority, parent_old, smooth_rate):
    nest = lax.axis_index("nest")
    depth = col_weights.shape[0]
    vmem = pl.BlockSpec(memory_space=pltpu.VMEM)
    smem = pl.BlockSpec(memory_space=pltpu.SMEM)
    f32 = jnp.float32
    shift = lax.dynamic_slice(nest_offsets, (nest, 1), (1, 1)).reshape(1)
    sent = pl.pallas_call(
        restrict_kernel,
        grid=(depth // DEPTH,),
        out_shape=jax.ShapeDtypeStruct((TILES, GROUPS, PR, LANES), f32),
        in_specs=[
            smem,
            pl.BlockSpec((32, 24, DEPTH), lambda k: (0, 0, k)),
            pl.BlockSpec((8, 24), lambda k: (0, 0)),
            pl.BlockSpec((DEPTH, 1024), lambda k: (k, 0)),
        ],
        out_specs=pl.BlockSpec((TILES, GROUPS, PR, LANES), lambda k: (0, 0, 0, 0)),
        scratch_shapes=[pltpu.VMEM((256, 1024), f32), pltpu.VMEM((256, 1024), f32)],
        name="restrict",
        compiler_params=pltpu.CompilerParams(dimension_semantics=("arbitrary",)),
    )(shift, child_fields[0], row_weights, col_weights)
    dma = pltpu.SemaphoreType.DMA
    return pl.pallas_call(
        exchange_kernel,
        out_shape=jax.ShapeDtypeStruct(parent_old.shape, f32),
        in_specs=[smem, smem, vmem, vmem, vmem],
        out_specs=vmem,
        scratch_shapes=[
            [pltpu.VMEM((NROWS + PR, LANES), f32)] * GROUPS,
            pltpu.VMEM((GROUPS, NROWS, LANES), f32),
            pltpu.VMEM((NESTS, GROUPS, OWN, LANES), f32),
            pltpu.VMEM((GROUPS, OWN, LANES), f32),
            pltpu.VMEM((OWN, LANES), f32),
            pltpu.VMEM((2, GROUPS, STRIP, LANES), f32),
            pltpu.VMEM((2, GROUPS, PR, LANES), f32),
            pltpu.VMEM((2, GROUPS, STRIP, LANES), f32),
            dma((GROUPS,)), dma((GROUPS,)), dma((GROUPS, NESTS)), dma((GROUPS, NESTS)),
            dma((GROUPS, 4)), dma((GROUPS, 4)),
        ],
        name="exchange",
        compiler_params=pltpu.CompilerParams(collective_id=0, has_side_effects=True),
    )(smooth_rate, nest_offsets, sent, priority, parent_old)


def solution(mesh):
    return jax.shard_map(
        per_device,
        mesh=mesh,
        in_specs=(
            P("nest", None, "tile", None), P(), P(), P(), P("tile", "nest"), P(None, "tile", "nest"), P(),
        ),
        out_specs=P(None, "tile", "nest"),
        check_vma=False,
    )
```

time: 147 us -> 75.4 us (0.51)
  the two profiles are of different devices: /device:TPU:32 before, /device:TPU:1 now
where the time goes in v1:
time: 75.4 us; the launch traced here: 74.4 us
  Pallas kernels  69.8 us (93%)
  local copies, waits for them, and re-layouts  4.54 us (6%)
    pallas_call x1, Pallas kernels, per_device(): pl.pallas_call(exchange_kernel, out_shape=jax.ShapeDtypeStruct(parent_old...  52.7 us
    pallas_call x1, Pallas kernels, per_device(): pl.pallas_call(restrict_kernel, grid=(depth // DEPTH,), out_shape=jax.Sha...  17.1 us
    unnamed x2, local copies, waits for them, and re-layouts  3.2 us

profile of v1, /device:TPU:1, one launch (start us, length us, event | category | flops | bytes accessed | tf_op | source)
XLA Modules:
  0.0 74.4 jit_solution(15343802776989512103)
XLA Ops:
  0.0 1.3 %constant_dynamic-slice_fusion = s32[1,1]{0,1:T(1,128)} fusion(s32[4,2]{0,1:T(2,128)} %param.10, s32[]{:T(128)S(6)} %select_n.3), kind=kLoop, calls=%fused_computation | loop fusion | bytes 12 | tf_op jit(solution)/shard_map/dynamic_slice | solution.py:237
  1.3 1.3 %copy.8.offsets_ref = s32[4,2]{1,0:T(4,128)} copy(s32[4,2]{0,1:T(2,128)} %param.10) | data formatting | bytes 64 | tf_op args[3]
  2.7 17.1 %restrict.1.sent = f32[64,4,8,128]{3,2,1,0:T(8,128)} custom-call(s32[1]{0:T(128)} %bitcast.shift_ref, f32[32,24,3072]{2,1,0:T(8,128)} %bitcast.2, f32[8,24]{1,0:T(8,128)} %rw_ref.1, f32[3072,1024]{1,0:T(8,128)} %cw_ref.1), custom_call_target="tpu_custom_call" | custom-call | tf_op jit(solution)/shard_map/restrict/pallas_call | solution.py:238
  19.8 52.7 %exchange.1 = f32[32,16,256]{2,1,0:T(8,128)} custom-call(f32[32]{0:T(128)} %rate_ref.1, s32[4,2]{1,0:T(4,128)} %copy.8.offsets_ref, f32[64,4,8,128]{3,2,1,0:T(8,128)} %restrict.1.sent, s32[16,256]{1,0:T(8,128)} %priority_ref.1, f32[32,16,256]{2,1,0:T(8,128)} %old_ref.1), custom_call_target="tpu_custom_call" | custom-call | tf_op jit(solution)/shard_map/exchange/pallas_call | solution.py:254
  72.5 1.9 %copy.10 = f32[32,16,256]{2,1,0:T(8,128)} copy(f32[32,16,256]{2,1,0:T(8,128)} %exchange.1) | data formatting | bytes 1048576

commit v2 on v1

--- a/solution.py
+++ b/solution.py
@@ -54,59 +54,67 @@
     return tiles
 
 
-def restrict_kernel(shift_ref, child_ref, rw_ref, cw_ref, out_ref, total, rolled):
-    step = pl.program_id(0)
-    w_high, w_low = split(rw_ref[...])
-    w_high, w_low = block_diagonal(w_high, GF), block_diagonal(w_low, GF)
-    thin = []
-    for g in range(GROUPS):
-        c_high, c_low = split(child_ref[pl.ds(g * GF, GF)].reshape(GF * 24, DEPTH))
-        thin.append(dot(w_high, c_high) + (dot(w_low, c_high) + dot(w_high, c_low)))
-    t_high, t_low = split(jnp.concatenate(thin, axis=0))
-    m_high, m_low = split(cw_ref[...])
-    part = dot(t_high, m_high) + (dot(t_low, m_high) + dot(t_high, m_low))
-
-    @pl.when(step == 0)
-    def _():
-        total[...] = part
-
-    @pl.when(step > 0)
-    def _():
-        total[...] += part
-
-    @pl.when(step == pl.num_programs(0) - 1)
-    def _():
-        rolled[...] = pltpu.roll(total[...], shift_ref[0], 1)
-
-        @pl.loop(0, GROUPS)
-        def _(g):
-            for z in range(8):
-                tiles = [
-                    rolled[pl.ds(pl.multiple_of((g * GF + f) * PR, PR), PR), z * LANES : (z + 1) * LANES]
-                    for f in range(GF)
-                ]
-                for s, tile in enumerate(regroup(tiles)):
-                    out_ref[z * 8 + s, g] = tile
-
-
-def exchange_kernel(
-    rate_ref, offsets_ref, sent, priority_ref, old_ref, out_ref,
+def restrict_half(h, shift, waits, child, weights, high, low, total, packed):
+    w_high, w_low = weights
+    for c in range(3):
+        waits[0][c].wait()
+        columns = slice(c * 1024, (c + 1) * 1024)
+        for g in range(2):
+            c_high, c_low = split(child[0][pl.ds(h * 16 + g * GF, GF), :, columns].reshape(GF * 24, 1024))
+            thin = dot(w_high, c_high) + (dot(w_low, c_high) + dot(w_high, c_low))
+            t_high, t_low = split(thin)
+            high[g * 64 : (g + 1) * 64, columns] = t_high
+            low[g * 64 : (g + 1) * 64, columns] = t_low
+    for k in range(3072 // DEPTH):
+        rows = slice(k * DEPTH, (k + 1) * DEPTH)
+        if waits[1]:
+            waits[1][k].wait()
+        m_high, m_low = split(child[1][rows, :])
+        part = dot(high[:, rows], m_high) + (dot(low[:, rows], m_high) + dot(high[:, rows], m_low))
+        if k == 0:
+            total[...] = part
+        else:
+            total[...] += part
+    total[...] = pltpu.roll(total[...], shift, 1)
+    for g in range(2):
+        for z in range(8):
+            tiles = [total[(g * GF + f) * PR : (g * GF + f + 1) * PR, z * LANES : (z + 1) * LANES] for f in range(GF)]
+            for s, tile in enumerate(regroup(tiles)):
+                packed[z * 8 + s, h * 2 + g] = tile
+
+
+def step_kernel(
+    rate_ref, offsets_ref, child_hbm, rw_ref, cw_hbm, priority_ref, old_ref, out_ref,
+    child, cw, high, low, total, sent,
     slabs, halves, nests, merged, mask, edges, rows_in, edges_in,
-    tile_send, tile_recv, nest_send, nest_recv, halo_send, halo_recv,
+    child_sem, cw_sem, tile_send, tile_recv, nest_send, nest_recv, halo_send, halo_recv,
 ):
     me, nest = lax.axis_index("tile"), lax.axis_index("nest")
     barrier = pltpu.get_barrier_semaphore()
 
+    def child_copy(h, c):
+        part = (pl.ds(h * 16, 16), slice(None), pl.ds(c * 1024, 1024))
+        return pltpu.make_async_copy(child_hbm.at[part], child.at[part], child_sem.at[h, c])
+
+    def cw_copy(k):
+        rows = pl.ds(k * DEPTH, DEPTH)
+        return pltpu.make_async_copy(cw_hbm.at[rows], cw.at[rows], cw_sem.at[k])
+
+    child_copies = [[child_copy(h, c) for c in range(3)] for h in range(2)]
+    cw_copies = [cw_copy(k) for k in range(3072 // DEPTH)]
+    for copy in child_copies[0] + cw_copies + child_copies[1]:
+        copy.start()
+
     @pl.loop(1, TILES)
     def _(d):
         pl.semaphore_signal(barrier, inc=1, device_id={"tile": lax.rem(me + d, TILES)}, device_id_type=MESH)
 
     for d in range(1, NESTS):
         pl.semaphore_signal(barrier, inc=1, device_id={"nest": lax.rem(nest + d, NESTS)}, device_id_type=MESH)
-    pl.semaphore_wait(barrier, TILES - 1 + NESTS - 1)
 
     own_rows = pl.ds(pl.multiple_of(me * PR, PR), PR)
-    for g in range(GROUPS):
+
+    def send_group(g):
         @pl.loop(1, TILES)
         def _(d):
             peer = lax.rem(me + d, TILES)
@@ -116,6 +124,17 @@
                 device_id={"tile": peer}, device_id_type=MESH,
             ).start()
 
+    shift = offsets_ref[1, nest]
+    r_high, r_low = split(rw_ref[...])
+    weights = block_diagonal(r_high, GF), block_diagonal(r_low, GF)
+    restrict_half(0, shift, (child_copies[0], cw_copies), (child, cw), weights, high, low, total, sent)
+    pl.semaphore_wait(barrier, TILES - 1 + NESTS - 1)
+    send_group(0)
+    send_group(1)
+    restrict_half(1, shift, (child_copies[1], None), (child, cw), weights, high, low, total, sent)
+    send_group(2)
+    send_group(3)
+
     for g in range(GROUPS):
         slabs[g][own_rows, :] = sent[me, g]
 
@@ -127,7 +146,7 @@
     def wait(ref, sem):
         pltpu.make_async_copy(ref, ref, sem).wait()
 
-    first = offsets_ref[nest, 0]
+    first = offsets_ref[0, nest]
     half = lax.rem(nest, 2)
 
     def nest_copy(g, d):
@@ -139,16 +158,13 @@
             device_id={"nest": peer}, device_id_type=MESH,
         )
 
-    for g in range(GROUPS):
-        wait(slabs[g].at[pl.ds(0, NROWS - PR)], tile_recv.at[g])
+    def shift_rows(g):
         slab = slabs[g]
+        wait(slab.at[pl.ds(0, NROWS - PR)], tile_recv.at[g])
         slab[NROWS : NROWS + PR, :] = slab[0:PR, :]
-
-        @pl.loop(0, NROWS // PR)
-        def _(b):
+        for b in range(NROWS // PR):
             start = (b * PR - first) & (NROWS - 1)
-            halves[g, pl.ds(pl.multiple_of(b * PR, PR), PR), :] = slab[pl.ds(start, PR), :]
-
+            halves[g, b * PR : (b + 1) * PR, :] = slab[pl.ds(start, PR), :]
         for d in range(1, NESTS):
             nest_copy(g, d).start()
         nests[nest, g] = halves[g, pl.ds(pl.multiple_of(half * OWN, OWN), OWN), :]
@@ -171,7 +187,7 @@
             copy(merged.at[g, pl.ds(0, PR)], rows_in.at[1, g], 3, {"nest": below}),
         ]
 
-    for g in range(GROUPS):
+    def merge(g):
         for d in range(1, NESTS):
             nest_copy(g, d).wait_recv()
         high = jnp.zeros((STRIP, LANES), jnp.float32)
@@ -195,7 +211,7 @@
     wide = lax.broadcasted_iota(jnp.int32, (OWN, LANES), 1)
     wide_column = wide % STRIP
     row = lax.broadcasted_iota(jnp.int32, (OWN, LANES), 0)
-    for g in range(GROUPS):
+    def smooth(g):
         copies = halo_copies(g)
         for copy in copies:
             copy.wait_recv()
@@ -221,6 +237,16 @@
         out_ref[pl.ds(g * GF, GF)] = new.T.reshape(GF, STRIP, OWN)
 
     for g in range(GROUPS):
+        shift_rows(g)
+        if g >= 1:
+            merge(g - 1)
+        if g >= 2:
+            smooth(g - 2)
+    merge(GROUPS - 1)
+    smooth(GROUPS - 2)
+    smooth(GROUPS - 1)
+
+    for g in range(GROUPS):
         wait(slabs[g].at[pl.ds(0, NROWS - PR)], tile_send.at[g])
         for d in range(1, NESTS):
             nest_copy(g, d).wait_send()
@@ -229,34 +255,23 @@
 
 
 def per_device(child_fields, row_weights, col_weights, nest_offsets, priority, parent_old, smooth_rate):
-    nest = lax.axis_index("nest")
-    depth = col_weights.shape[0]
     vmem = pl.BlockSpec(memory_space=pltpu.VMEM)
     smem = pl.BlockSpec(memory_space=pltpu.SMEM)
-    f32 = jnp.float32
-    shift = lax.dynamic_slice(nest_offsets, (nest, 1), (1, 1)).reshape(1)
-    sent = pl.pallas_call(
-        restrict_kernel,
-        grid=(depth // DEPTH,),
-        out_shape=jax.ShapeDtypeStruct((TILES, GROUPS, PR, LANES), f32),
-        in_specs=[
-            smem,
-            pl.BlockSpec((32, 24, DEPTH), lambda k: (0, 0, k)),
-            pl.BlockSpec((8, 24), lambda k: (0, 0)),
-            pl.BlockSpec((DEPTH, 1024), lambda k: (k, 0)),
-        ],
-        out_specs=pl.BlockSpec((TILES, GROUPS, PR, LANES), lambda k: (0, 0, 0, 0)),
-        scratch_shapes=[pltpu.VMEM((256, 1024), f32), pltpu.VMEM((256, 1024), f32)],
-        name="restrict",
-        compiler_params=pltpu.CompilerParams(dimension_semantics=("arbitrary",)),
-    )(shift, child_fields[0], row_weights, col_weights)
+    hbm = pl.BlockSpec(memory_space=pl.ANY)
+    f32, bf16 = jnp.float32, jnp.bfloat16
     dma = pltpu.SemaphoreType.DMA
     return pl.pallas_call(
-        exchange_kernel,
+        step_kernel,
         out_shape=jax.ShapeDtypeStruct(parent_old.shape, f32),
-        in_specs=[smem, smem, vmem, vmem, vmem],
+        in_specs=[smem, smem, hbm, vmem, hbm, vmem, vmem],
         out_specs=vmem,
         scratch_shapes=[
+            pltpu.VMEM((32, 24, 3072), f32),
+            pltpu.VMEM((3072, 1024), f32),
+            pltpu.VMEM((128, 3072), bf16),
+            pltpu.VMEM((128, 3072), bf16),
+            pltpu.VMEM((128, 1024), f32),
+            pltpu.VMEM((TILES, GROUPS, PR, LANES), f32),
             [pltpu.VMEM((NROWS + PR, LANES), f32)] * GROUPS,
             pltpu.VMEM((GROUPS, NROWS, LANES), f32),
             pltpu.VMEM((NESTS, GROUPS, OWN, LANES), f32),
@@ -265,12 +280,13 @@
             pltpu.VMEM((2, GROUPS, STRIP, LANES), f32),
             pltpu.VMEM((2, GROUPS, PR, LANES), f32),
             pltpu.VMEM((2, GROUPS, STRIP, LANES), f32),
+            dma((2, 3)), dma((3072 // DEPTH,)),
             dma((GROUPS,)), dma((GROUPS,)), dma((GROUPS, NESTS)), dma((GROUPS, NESTS)),
             dma((GROUPS, 4)), dma((GROUPS, 4)),
         ],
-        name="exchange",
+        name="feedback",
         compiler_params=pltpu.CompilerParams(collective_id=0, has_side_effects=True),
-    )(smooth_rate, nest_offsets, sent, priority, parent_old)
+    )(smooth_rate, nest_offsets.T, child_fields[0], row_weights, col_weights, priority, parent_old)
 
 
 def solution(mesh):

time: 75.4 us -> 58.9 us (0.78); the launches traced: 74.4 us -> 58.7 us
  Pallas kernels: 69.8 us -> 56.8 us
  local copies, waits for them, and re-layouts: 4.54 us -> 1.87 us
    pallas_call x2 -> x1, Pallas kernels: 69.8 us -> 56.8 us  [per_device(): pl.pallas_call(step_kernel, out_shape=jax.ShapeDtypeStruct(parent_old.sha...]
    dynamic_slice x1 -> x0, local copies, waits for them, and re-layouts: 1.34 us -> none  [per_device(): shift = lax.dynamic_slice(nest_offsets, (nest, 1), (1, 1)).reshape(1)]
    unnamed x2 -> x1, local copies, waits for them, and re-layouts: 3.2 us -> 1.87 us
where the time goes in v2:
time: 58.9 us; the launch traced here: 58.7 us
  Pallas kernels  56.8 us (96%)
  local copies, waits for them, and re-layouts  1.87 us (3%)
    pallas_call x1, Pallas kernels, per_device(): pl.pallas_call(step_kernel, out_shape=jax.ShapeDtypeStruct(parent_old.sha...  56.8 us
    unnamed x1, local copies, waits for them, and re-layouts  1.87 us

profile of v2, /device:TPU:1, one launch (start us, length us, event | category | flops | bytes accessed | tf_op | source)
XLA Modules:
  0.0 58.7 jit_solution(10908634332724836832)
XLA Ops:
  0.0 56.8 %feedback.1 = f32[32,16,256]{2,1,0:T(8,128)} custom-call(f32[32]{0:T(128)} %rate_ref.1, s32[2,4]{1,0:T(2,128)} %bitcast.3, f32[32,24,3072]{2,1,0:T(8,128)} %bitcast.2, f32[8,24]{1,0:T(8,128)} %rw_ref.1, f32[3072,1024]{1,0:T(8,128)} %cw_hbm.1, s32[16,256]{1,0:T(8,128)} %priority_ref.1, f32[32,16,256]{2,1,0:T(8,128)} %old_ref.1), custom_call_target="tpu_custom_call" | custom-call | tf_op jit(solution)/shard_map/feedback/pallas_call | solution.py:263
  56.9 1.9 %copy.9 = f32[32,16,256]{2,1,0:T(8,128)} copy(f32[32,16,256]{2,1,0:T(8,128)} %feedback.1) | data formatting | bytes 1048576

commit v3 on v2

--- a/solution.py
+++ b/solution.py
@@ -14,10 +14,12 @@
 GF = 8
 PR = 8
 STRIP = 16
+PASSES = ((0,), (1,), (2, 3))
 LANES = 128
 NROWS = 512
 OWN = 256
 DEPTH = 512
+CHUNKS = tuple((k, 512) for k in range(0, 3072, 512))
 
 
 def split(value):
@@ -54,55 +56,66 @@
     return tiles
 
 
-def restrict_half(h, shift, waits, child, weights, high, low, total, packed):
-    w_high, w_low = weights
+def restrict(groups, shift, child_waits, cw_waits, child, cw, weights, both, total, packed):
+    count = len(groups) * GF * PR
     for c in range(3):
-        waits[0][c].wait()
         columns = slice(c * 1024, (c + 1) * 1024)
-        for g in range(2):
-            c_high, c_low = split(child[0][pl.ds(h * 16 + g * GF, GF), :, columns].reshape(GF * 24, 1024))
-            thin = dot(w_high, c_high) + (dot(w_low, c_high) + dot(w_high, c_low))
-            t_high, t_low = split(thin)
-            high[g * 64 : (g + 1) * 64, columns] = t_high
-            low[g * 64 : (g + 1) * 64, columns] = t_low
-    for k in range(3072 // DEPTH):
-        rows = slice(k * DEPTH, (k + 1) * DEPTH)
-        if waits[1]:
-            waits[1][k].wait()
-        m_high, m_low = split(child[1][rows, :])
-        part = dot(high[:, rows], m_high) + (dot(low[:, rows], m_high) + dot(high[:, rows], m_low))
-        if k == 0:
-            total[...] = part
+        for i, g in enumerate(groups):
+            child_waits[g][c].wait()
+            c_high, c_low = split(child[pl.ds(g * GF, GF), :, columns].reshape(GF * 24, 1024))
+            wide = dot(weights, c_high)
+            t_high, t_low = split(wide[:64] + (wide[64:] + dot(weights[:64], c_low)))
+            both[i * 64 : (i + 1) * 64, columns] = t_high
+            both[count + i * 64 : count + (i + 1) * 64, columns] = t_low
+    for start, depth in CHUNKS:
+        rows = slice(start, start + depth)
+        for copy, low, _ in cw_waits:
+            if start <= low < start + depth:
+                copy.wait()
+        m_high, m_low = split(cw[rows, :])
+        wide = dot(both[0 : 2 * count, rows], m_high)
+        part = wide[:count] + (wide[count:] + dot(both[0:count, rows], m_low))
+        if start == 0:
+            total[0:count, :] = part
         else:
-            total[...] += part
-    total[...] = pltpu.roll(total[...], shift, 1)
-    for g in range(2):
+            total[0:count, :] += part
+    total[0:count, :] = pltpu.roll(total[0:count, :], shift, 1)
+    for i, g in enumerate(groups):
         for z in range(8):
-            tiles = [total[(g * GF + f) * PR : (g * GF + f + 1) * PR, z * LANES : (z + 1) * LANES] for f in range(GF)]
+            tiles = [total[(i * GF + f) * PR : (i * GF + f + 1) * PR, z * LANES : (z + 1) * LANES] for f in range(GF)]
             for s, tile in enumerate(regroup(tiles)):
-                packed[z * 8 + s, h * 2 + g] = tile
+                packed[z * 8 + s, g] = tile
 
 
 def step_kernel(
-    rate_ref, offsets_ref, child_hbm, rw_ref, cw_hbm, priority_ref, old_ref, out_ref,
-    child, cw, high, low, total, sent,
+    rate_hbm, offsets_hbm, child_hbm, rw_hbm, cw_hbm, priority_hbm, old_hbm, out_hbm,
+    child, cw, both, total, sent, priority_ref, old_ref, out_ref, rate_ref, offsets_ref, rw_ref,
     slabs, halves, nests, merged, mask, edges, rows_in, edges_in,
-    child_sem, cw_sem, tile_send, tile_recv, nest_send, nest_recv, halo_send, halo_recv,
+    child_sem, cw_sem, own_sem, out_sem, tile_send, tile_recv, nest_send, nest_recv, halo_send, halo_recv,
 ):
     me, nest = lax.axis_index("tile"), lax.axis_index("nest")
     barrier = pltpu.get_barrier_semaphore()
 
-    def child_copy(h, c):
-        part = (pl.ds(h * 16, 16), slice(None), pl.ds(c * 1024, 1024))
-        return pltpu.make_async_copy(child_hbm.at[part], child.at[part], child_sem.at[h, c])
+    def child_copy(g, c):
+        part = (pl.ds(g * GF, GF), slice(None), pl.ds(c * 1024, 1024))
+        return pltpu.make_async_copy(child_hbm.at[part], child.at[part], child_sem.at[g, c])
 
     def cw_copy(k):
         rows = pl.ds(k * DEPTH, DEPTH)
         return pltpu.make_async_copy(cw_hbm.at[rows], cw.at[rows], cw_sem.at[k])
 
-    child_copies = [[child_copy(h, c) for c in range(3)] for h in range(2)]
+    child_copies = [[child_copy(g, c) for c in range(3)] for g in range(GROUPS)]
     cw_copies = [cw_copy(k) for k in range(3072 // DEPTH)]
-    for copy in child_copies[0] + cw_copies + child_copies[1]:
+    own_copies = [
+        pltpu.make_async_copy(priority_hbm, priority_ref, own_sem.at[0]),
+        pltpu.make_async_copy(old_hbm, old_ref, own_sem.at[1]),
+    ]
+    rate_copy = pltpu.make_async_copy(rate_hbm, rate_ref, own_sem.at[2])
+    offsets_copy = pltpu.make_async_copy(offsets_hbm, offsets_ref, own_sem.at[3])
+    rw_copy = pltpu.make_async_copy(rw_hbm, rw_ref, own_sem.at[4])
+    for copy in (rw_copy, offsets_copy, rate_copy):
+        copy.start()
+    for copy in child_copies[0] + cw_copies + sum(child_copies[1:], own_copies):
         copy.start()
 
     @pl.loop(1, TILES)
@@ -114,30 +127,44 @@
 
     own_rows = pl.ds(pl.multiple_of(me * PR, PR), PR)
 
+    plane, seat = lax.div(me, 8), lax.rem(me, 8)
+
+    def send_tile(g, peer):
+        pltpu.make_async_remote_copy(
+            src_ref=sent.at[peer, g], dst_ref=slabs[g].at[own_rows],
+            send_sem=tile_send.at[g], recv_sem=tile_recv.at[g],
+            device_id={"tile": peer}, device_id_type=MESH,
+        ).start()
+
     def send_group(g):
-        @pl.loop(1, TILES)
+        @pl.loop(0, 8)
         def _(d):
-            peer = lax.rem(me + d, TILES)
-            pltpu.make_async_remote_copy(
-                src_ref=sent.at[peer, g], dst_ref=slabs[g].at[own_rows],
-                send_sem=tile_send.at[g], recv_sem=tile_recv.at[g],
-                device_id={"tile": peer}, device_id_type=MESH,
-            ).start()
-
+            for dz in (4, 3, 5, 2, 6, 1, 7):
+                send_tile(g, lax.rem(plane + dz, 8) * 8 + lax.rem(seat + d, 8))
+
+        @pl.loop(1, 8)
+        def _(d):
+            send_tile(g, plane * 8 + lax.rem(seat + d, 8))
+
+    for copy in (rw_copy, offsets_copy, rate_copy):
+        copy.wait()
     shift = offsets_ref[1, nest]
     r_high, r_low = split(rw_ref[...])
-    weights = block_diagonal(r_high, GF), block_diagonal(r_low, GF)
-    restrict_half(0, shift, (child_copies[0], cw_copies), (child, cw), weights, high, low, total, sent)
-    pl.semaphore_wait(barrier, TILES - 1 + NESTS - 1)
-    send_group(0)
-    send_group(1)
-    restrict_half(1, shift, (child_copies[1], None), (child, cw), weights, high, low, total, sent)
-    send_group(2)
-    send_group(3)
+    weights = jnp.concatenate([block_diagonal(r_high, GF), block_diagonal(r_low, GF)], axis=0)
+    cw_waits = [(copy, k * DEPTH, (k + 1) * DEPTH) for k, copy in enumerate(cw_copies)]
+    for groups in PASSES:
+        restrict(groups, shift, child_copies, cw_waits, child, cw, weights, both, total, sent)
+        if groups[0] == 0:
+            pl.semaphore_wait(barrier, TILES - 1 + NESTS - 1)
+        cw_waits = []
+        for g in groups:
+            send_group(g)
 
     for g in range(GROUPS):
         slabs[g][own_rows, :] = sent[me, g]
 
+    for copy in own_copies:
+        copy.wait()
     spread = jnp.concatenate([priority_ref[...].astype(jnp.float32)] * GF, axis=0)
     mask[...] = spread.T
     for g in range(GROUPS):
@@ -157,6 +184,10 @@
             send_sem=nest_send.at[g, d], recv_sem=nest_recv.at[g, d],
             device_id={"nest": peer}, device_id_type=MESH,
         )
+
+    def out_copy(g):
+        part = pl.ds(g * GF, GF)
+        return pltpu.make_async_copy(out_ref.at[part], out_hbm.at[part], out_sem.at[g])
 
     def shift_rows(g):
         slab = slabs[g]
@@ -235,6 +266,7 @@
             rate = jnp.where(wide[0:1] // STRIP == f, rate_ref[g * GF + f], rate)
         new = cell + rate * (east_side + west_side + north_side + south_side - 4.0 * cell)
         out_ref[pl.ds(g * GF, GF)] = new.T.reshape(GF, STRIP, OWN)
+        out_copy(g).start()
 
     for g in range(GROUPS):
         shift_rows(g)
@@ -242,8 +274,8 @@
             merge(g - 1)
         if g >= 2:
             smooth(g - 2)
+    smooth(GROUPS - 2)
     merge(GROUPS - 1)
-    smooth(GROUPS - 2)
     smooth(GROUPS - 1)
 
     for g in range(GROUPS):
@@ -252,26 +284,30 @@
             nest_copy(g, d).wait_send()
         for copy in halo_copies(g):
             copy.wait_send()
+        out_copy(g).wait()
 
 
 def per_device(child_fields, row_weights, col_weights, nest_offsets, priority, parent_old, smooth_rate):
-    vmem = pl.BlockSpec(memory_space=pltpu.VMEM)
-    smem = pl.BlockSpec(memory_space=pltpu.SMEM)
     hbm = pl.BlockSpec(memory_space=pl.ANY)
     f32, bf16 = jnp.float32, jnp.bfloat16
     dma = pltpu.SemaphoreType.DMA
     return pl.pallas_call(
         step_kernel,
         out_shape=jax.ShapeDtypeStruct(parent_old.shape, f32),
-        in_specs=[smem, smem, hbm, vmem, hbm, vmem, vmem],
-        out_specs=vmem,
+        in_specs=[hbm] * 7,
+        out_specs=hbm,
         scratch_shapes=[
             pltpu.VMEM((32, 24, 3072), f32),
             pltpu.VMEM((3072, 1024), f32),
-            pltpu.VMEM((128, 3072), bf16),
-            pltpu.VMEM((128, 3072), bf16),
+            pltpu.VMEM((256, 3072), bf16),
             pltpu.VMEM((128, 1024), f32),
             pltpu.VMEM((TILES, GROUPS, PR, LANES), f32),
+            pltpu.VMEM((STRIP, OWN), jnp.int32),
+            pltpu.VMEM((32, STRIP, OWN), f32),
+            pltpu.VMEM((32, STRIP, OWN), f32),
+            pltpu.SMEM((32,), f32),
+            pltpu.SMEM((2, 4), jnp.int32),
+            pltpu.VMEM((8, 24), f32),
             [pltpu.VMEM((NROWS + PR, LANES), f32)] * GROUPS,
             pltpu.VMEM((GROUPS, NROWS, LANES), f32),
             pltpu.VMEM((NESTS, GROUPS, OWN, LANES), f32),
@@ -280,7 +316,7 @@
             pltpu.VMEM((2, GROUPS, STRIP, LANES), f32),
             pltpu.VMEM((2, GROUPS, PR, LANES), f32),
             pltpu.VMEM((2, GROUPS, STRIP, LANES), f32),
-            dma((2, 3)), dma((3072 // DEPTH,)),
+            dma((GROUPS, 3)), dma((3072 // DEPTH,)), dma((5,)), dma((GROUPS,)),
             dma((GROUPS,)), dma((GROUPS,)), dma((GROUPS, NESTS)), dma((GROUPS, NESTS)),
             dma((GROUPS, 4)), dma((GROUPS, 4)),
         ],

time: 58.9 us -> 57.2 us (0.971)
  Pallas kernels: 56.8 us -> 55.2 us
    pallas_call x1, Pallas kernels: 56.8 us -> 55.2 us  [per_device(): pl.pallas_call(step_kernel, out_shape=jax.ShapeDtypeStruct(parent_old.sha...]
where the time goes in v3:
time: 57.2 us; the launch traced here: 57 us
  Pallas kernels  55.2 us (97%)
  local copies, waits for them, and re-layouts  1.87 us (3%)
    pallas_call x1, Pallas kernels, per_device(): pl.pallas_call(step_kernel, out_shape=jax.ShapeDtypeStruct(parent_old.sha...  55.2 us
    unnamed x1, local copies, waits for them, and re-layouts  1.87 us

profile of v3, /device:TPU:1, one launch (start us, length us, event | category | flops | bytes accessed | tf_op | source)
XLA Modules:
  0.0 57.0 jit_solution(1944081800999616320)
XLA Ops:
  0.0 55.2 %feedback.1 = f32[32,16,256]{2,1,0:T(8,128)} custom-call(f32[32]{0:T(128)} %rate_hbm.1, s32[2,4]{1,0:T(2,128)} %bitcast.3, f32[32,24,3072]{2,1,0:T(8,128)} %bitcast.2, f32[8,24]{1,0:T(8,128)} %rw_hbm.1, f32[3072,1024]{1,0:T(8,128)} %cw_hbm.1, s32[16,256]{1,0:T(8,128)} %priority_hbm.1, f32[32,16,256]{2,1,0:T(8,128)} %old_hbm.1), custom_call_target="tpu_custom_call" | custom-call | tf_op jit(solution)/shard_map/feedback/pallas_call | solution.py:294
  55.2 1.9 %copy.9 = f32[32,16,256]{2,1,0:T(8,128)} copy(f32[32,16,256]{2,1,0:T(8,128)} %feedback.1) | data formatting | bytes 1048576
